TPU v7x, 32 devices: a whole 2x2x4 slice. The times are simulated.
32 devices in a mesh: tile: 8 (over z, x), mem: 4 (over y, core).
Axes of the slice: x: 2, y: 2, z: 4, core: 2. Of those that a mesh axis runs over, the one named last changes fastest.
Arguments:
- footprints: bfloat16 [1024, 128, 128], P('tile'), may hold values from -0.1875 to 0.1875
- tile_row: int32 [1024], P('tile'), may hold values from 0 to 127, as said below
- tile_col: int32 [1024], P('tile'), may hold values from 0 to 63, as said below
- prior_flux: bfloat16 [256, 8192], P('mem', 'tile'), may hold values from -12 to 12
- observed: float32 [256, 16384], P('mem', 'tile'), may hold values from -6 to 6
- precision_weight: int32 [16384], P('tile'), may hold values from 1 to 16
Outputs:
- gradient: float32 [256, 8192], P('mem', 'tile')
Inputs may be any that keep to these rules, and one draw needn't show every extreme that they name: Among the 128 tiles of each index of tile, at most 24 have a row block of one owner (owner = tile_row // 16); in every draw one owner gets exactly 24 from every index. Likewise with owner = tile_col // 8: at most 24 from one index of tile to one owner, and one owner gets exactly 24 from every index.
All inputs are finite; a program needn't handle non-finite values.
Results may differ from a plain program's by a relative error of at most 0.0052.
Values may be sent and summed in bfloat16 or wider, within the bound.
No kernel may reach another device: no remote copies, remote signals or barrier semaphores. Data moves between devices by JAX's collectives and lax.ppermute only.
A program may use at most 64 MiB of HBM per device.

v0:
```python
import jax
import jax.numpy as jnp
from jax import lax
from jax.sharding import PartitionSpec as P

MEMBERS = 256
FLUX_DEV = 8
SOUND_DEV = 16


def slot_of(owners, capacity):
    entries = owners.shape[0]
    position = jnp.arange(entries)
    earlier = (owners[:, None] == owners[None, :]) & (position[None, :] < position[:, None])
    return owners * capacity + jnp.sum(earlier.astype(jnp.int32), axis=1)


def invert(slot_ids, slot_total):
    matches = slot_ids[None, :] == jnp.arange(slot_total)[:, None]
    sources = jnp.sum(jnp.where(matches, jnp.arange(slot_ids.shape[0])[None, :], 0), axis=1)
    return (sources, jnp.any(matches, axis=1))


def to_slots(values, sources, usage_flags):
    placed = jnp.take(values, sources, axis=1)
    return jnp.where(usage_flags[None, :, None], placed, jnp.zeros_like(placed))


def body(footprints, tile_row, tile_col, prior_flux, observed, precision_weight):
    devices_tile = lax.axis_size("tile")
    tile_count = footprints.shape[0]
    tile_size = footprints.shape[1]
    capacity = tile_count // devices_tile + max(1, tile_count // (2 * devices_tile))
    slot_total = devices_tile * capacity
    local_members = prior_flux.shape[0]
    local_sum = jnp.sum(prior_flux.astype(jnp.float32), axis=0)
    ensemble_sum = lax.psum(local_sum, "mem")
    ensemble_mean = ensemble_sum / MEMBERS
    member_deviations = (prior_flux.astype(jnp.float32) - ensemble_mean[None, :]).astype(
        jnp.bfloat16
    )
    row_owner = tile_row // SOUND_DEV
    row_local = tile_row % SOUND_DEV
    row_slot = slot_of(row_owner, capacity)
    row_source, row_used = invert(row_slot, slot_total)
    gathered = lax.all_gather(member_deviations, "tile", axis=1, tiled=True)
    retrieved_blocks = jnp.take(gathered.reshape(local_members, -1, tile_size), tile_col, axis=1)
    forward_terms = jnp.einsum(
        "mtk,trk->mtr", retrieved_blocks, footprints, preferred_element_type=jnp.float32
    )
    row_index = jnp.where(row_used, jnp.take(row_local, row_source), SOUND_DEV)
    sent_terms = to_slots(forward_terms, row_source, row_used)
    got_terms, got_rows = (
        lax.all_to_all(sent_terms, "tile", split_axis=1, concat_axis=1, tiled=True),
        lax.all_to_all(row_index[None, :], "tile", split_axis=1, concat_axis=1, tiled=True),
    )
    got_rows = got_rows[0]
    row_match = (got_rows[None, :] == jnp.arange(SOUND_DEV)[:, None]).astype(jnp.float32)
    modelled = jnp.einsum("ds,msk->mdk", row_match, got_terms, precision=lax.Precision.HIGHEST)
    targets = observed.reshape(local_members, SOUND_DEV, tile_size)
    obs_weight = (precision_weight.astype(jnp.float32) / 8.0).reshape(SOUND_DEV, tile_size)
    weighted = (obs_weight[None, :, :] * (modelled - targets)).astype(jnp.bfloat16)
    reply_rows = jnp.take(weighted, jnp.minimum(got_rows, SOUND_DEV - 1), axis=1)
    returned = lax.all_to_all(reply_rows, "tile", split_axis=1, concat_axis=1, tiled=True)
    residual_tiles = jnp.take(returned, row_slot, axis=1)
    backward_terms = jnp.einsum(
        "mtr,trk->mtk", residual_tiles, footprints, preferred_element_type=jnp.float32
    )
    picked = (tile_col[None, :] == jnp.arange(lax.axis_size("tile") * FLUX_DEV)[:, None]).astype(
        jnp.float32
    )
    reduced_total = lax.psum_scatter(
        jnp.einsum("ct,mtk->cmk", picked, backward_terms, precision=lax.Precision.HIGHEST),
        "tile",
        scatter_dimension=0,
        tiled=True,
    )
    gradient = reduced_total.transpose(1, 0, 2).reshape(local_members, FLUX_DEV * tile_size)
    return gradient


def solution(mesh):
    in_specs = (
        P("tile", None, None),
        P("tile"),
        P("tile"),
        P("mem", "tile"),
        P("mem", "tile"),
        P("tile"),
    )
    out_specs = P("mem", "tile")
    return jax.shard_map(body, mesh=mesh, in_specs=in_specs, out_specs=out_specs, check_vma=False)
```

profile of v0, /device:TPU:0, one launch (start us, length us, event | category | flops | bytes accessed | tf_op | source)
XLA Modules:
  0.0 394.9 jit_solution(9114734959783431947)
XLA Ops:
  6.5 0.9 convert_reduce_fusion
  7.5 8.4 %psum.7 = f32[1024]{0:T(1024)S(1)} all-reduce(f32[1024]{0:T(1024)S(1)} %convert_reduce_fusion), channel_id=1, replica_groups=mesh['tile'=8,'mem'=4] {'mem'}, use_global_device_ids=true, to_apply=%region_4.5 | all-reduce | flops 1024 | bytes 8192 | tf_op jit(solution)/shard_map/psum | solution.py:37
  15.9 1.6 fusion.24
  18.6 1.6 gather_fusion
  21.0 5.8 %all-to-all-start = ((s32[1,8,24]{2,0,1:T(1,128)}), s32[1,8,24]{2,0,1:T(1,128)S(1)}, u32[]{:S(2)}, u32[]{:S(2)}) async-start(s32[1,8,24]{2,0,1:T(1,128)} %bitcast.3), calls=%async_computation | async-start | bytes 8192 | tf_op jit(solution)/shard_map/all_to_all | solution.py:55
  28.2 30.0 %all-gather.2.cloned.1.call-done = bf16[64,8192]{1,0:T(8,128)(2,1)} async-done(((bf16[64,1024]{1,0:T(8,128)(2,1)}), bf16[64,8192]{1,0:T(8,128)(2,1)}) %all-gather.2.cloned.1.call-update) | async-done | bytes 1048592 | tf_op jit(solution)/shard_map/all_gather | solution.py:46
  58.2 1.5 copy_bitcast_fusion
  59.7 1.0 gather_fusion.1
  60.7 7.0 %convolution_bitcast_fusion.1 = f32[64,128,128]{2,0,1:T(8,128)} fusion(bf16[128,128,128]{2,1,0:T(8,128)(2,1)} %param.6, bf16[128,64,128]{2,1,0:T(8,128)(2,1)S(1)} %gather_fusion.1, pred[128]{0:T(512)(128)(4,1)S(1)} %compare_and_fusion), kind=kOutput, calls=%fused_computation.12 | convolution fusion | flops 269484032 | bytes 10485888 | tf_op jit(solution)/shard_map/mtk,trk->mtr/dot_general | solution.py:48
  67.7 5.8 %gather_fusion.2 = f32[192,64,128]{2,1,0:T(8,128)} fusion(f32[64,128,128]{2,0,1:T(8,128)} %convolution_bitcast_fusion.1, s32[1024]{0:T(1024)S(1)} %pad_clamp_fusion.3), kind=kCustom, calls=%fused_computation.2 | custom fusion | bytes 12583680 | tf_op jit(solution)/shard_map/jit(_take)/gather | solution.py:25
  73.5 5.4 %select_bitcast_fusion = f32[64,192,128]{2,0,1:T(8,128)} fusion(f32[192,64,128]{2,1,0:T(8,128)} %gather_fusion.2, pred[192]{0:T(512)(128)(4,1)S(1)} %fusion.25, pred[192]{0:T(512)(128)(4,1)S(1)} %compare_and_fusion.1), kind=kLoop, calls=%fused_computation.7 | loop fusion | flops 3145728 | bytes 12583296 | tf_op jit(solution)/shard_map/jit(_where)/select_n | solution.py:26
  79.0 4.9 %all-to-all-start.1 = ((f32[64,192,128]{2,0,1:T(8,128)}), f32[64,192,128]{2,0,1:T(8,128)}, u32[]{:S(2)}, u32[]{:S(2)}) async-start(f32[64,192,128]{2,0,1:T(8,128)} %select_bitcast_fusion), calls=%async_computation.1 | async-start | bytes 12582912 | tf_op jit(solution)/shard_map/all_to_all | solution.py:54
  84.5 0.7 minimum_reduce_fusion
  85.4 135.2 %all-to-all-done.1 = f32[64,192,128]{2,0,1:T(8,128)} async-done(((f32[64,192,128]{2,0,1:T(8,128)}), f32[64,192,128]{2,0,1:T(8,128)}, u32[]{:S(2)}, u32[]{:S(2)}) %all-to-all-start.1) | async-done | bytes 6291488 | tf_op jit(solution)/shard_map/all_to_all | solution.py:54
  220.6 8.1 %fusion.19 = bf16[64,16,128]{2,1,0:T(8,128)(2,1)S(1)} fusion(f32[64,16,128]{2,1,0:T(8,128)S(1)} %bitcast.49, f32[64,192,128]{2,0,1:T(8,128)} %all-to-all-done.1, f32[16,128]{1,0:T(8,128)S(1)} %multiply_bitcast_fusion, s32[192]{0:T(256)S(1)} %squeeze.3), kind=kOutput, calls=%fused_computation.22 | convolution fusion | flops 302386176 | bytes 7086848 | tf_op jit(solution)/shard_map/ds,msk->mdk/dot_general | solution.py:59
  228.7 1.2 gather_fusion.3
  229.9 2.1 select_bitcast_fusion.1
  232.0 3.6 all-to-all-start.2
  235.7 70.8 %all-to-all-done.2 = bf16[64,192,128]{2,0,1:T(8,128)(2,1)S(1)} async-done(((bf16[64,192,128]{2,0,1:T(8,128)(2,1)}), bf16[64,192,128]{2,0,1:T(8,128)(2,1)S(1)}, u32[]{:S(2)}, u32[]{:S(2)}) %all-to-all-start.2) | async-done | bytes 3145760 | tf_op jit(solution)/shard_map/all_to_all | solution.py:64
  306.5 2.2 gather_fusion.4
  308.7 4.1 %convolution_bitcast_fusion = f32[64,128,128]{2,0,1:T(8,128)S(1)} fusion(bf16[128,128,128]{2,1,0:T(8,128)(2,1)} %param.6, bf16[128,64,128]{2,1,0:T(8,128)(2,1)} %gather_fusion.4, pred[128]{0:T(512)(128)(4,1)S(1)} %get-tuple-element.7), kind=kOutput, calls=%fused_computation.11 | convolution fusion | flops 269484032 | bytes 10485888 | tf_op jit(solution)/shard_map/mtr,trk->mtk/dot_general | solution.py:66
  312.8 5.4 %fusion.2 = f32[64,64,128]{2,0,1:T(8,128)} fusion(f32[64,128,128]{2,0,1:T(8,128)S(1)} %convolution_bitcast_fusion, s32[128]{0:T(128)S(1)} %copy-done.2), kind=kOutput, calls=%fused_computation.8 | convolution fusion | flops 805314560 | bytes 6291968 | tf_op jit(solution)/shard_map/ct,mtk->cmk/dot_general | solution.py:73
  318.3 68.2 %reduce-scatter.2.cloned.1.call-done = f32[8,64,128]{2,0,1:T(8,128)} async-done(((f32[64,64,128]{2,0,1:T(8,128)}), f32[8,64,128]{2,0,1:T(8,128)}) %reduce-scatter.2.cloned.1.call-update) | async-done | bytes 262160 | tf_op jit(solution)/shard_map/reduce_scatter | solution.py:72
  386.4 1.7 copy.42
  (38 shorter events, 4.3 us)
Async XLA Ops:
  6.5 51.7 %all-gather.2.cloned.1.call-start = ((), (), s32[]{:S(2)}) async-start(), calls=%async_computation.4 | async-start | bytes 1179648 | tf_op jit(solution)/shard_map/all_gather | solution.py:46
  21.0 57.9 %all-to-all-start = ((s32[1,8,24]{2,0,1:T(1,128)}), s32[1,8,24]{2,0,1:T(1,128)S(1)}, u32[]{:S(2)}, u32[]{:S(2)}) async-start(s32[1,8,24]{2,0,1:T(1,128)} %bitcast.3), calls=%async_computation | async-start | bytes 8192 | tf_op jit(solution)/shard_map/all_to_all | solution.py:55
  79.0 4.9 %copy-start = (f32[64,2048]{1,0:T(8,128)S(1)}, f32[64,2048]{1,0:T(8,128)}, u32[]{:S(2)}) copy-start(f32[64,2048]{1,0:T(8,128)} %param.10) | copy-start | bytes 1572868
  79.0 5.0 %copy-start.1 = (s32[2048]{0:T(1024)S(1)}, s32[2048]{0:T(1024)}, u32[]{:S(2)}) copy-start(s32[2048]{0:T(1024)} %param.11) | copy-start | bytes 24580
  79.0 141.6 %all-to-all-start.1 = ((f32[64,192,128]{2,0,1:T(8,128)}), f32[64,192,128]{2,0,1:T(8,128)}, u32[]{:S(2)}, u32[]{:S(2)}) async-start(f32[64,192,128]{2,0,1:T(8,128)} %select_bitcast_fusion), calls=%async_computation.1 | async-start | bytes 12582912 | tf_op jit(solution)/shard_map/all_to_all | solution.py:54
  232.0 74.5 %all-to-all-start.2 = ((bf16[64,192,128]{2,0,1:T(8,128)(2,1)}), bf16[64,192,128]{2,0,1:T(8,128)(2,1)S(1)}, u32[]{:S(2)}, u32[]{:S(2)}) async-start(bf16[64,192,128]{2,0,1:T(8,128)(2,1)} %select_bitcast_fusion.1), calls=%async_computation.2 | async-start | bytes 6291456 | tf_op jit(solution)/shard_map/all_to_all | solution.py:64
  235.6 150.8 %reduce-scatter.2.cloned.1.call-start = ((), (), s32[]{:S(2)}) async-start(), calls=%async_computation.5 | async-start | bytes 2359296 | tf_op jit(solution)/shard_map/reduce_scatter | solution.py:72
  308.7 4.1 %copy-start.2 = (s32[128]{0:T(128)S(1)}, s32[128]{0:T(128)}, u32[]{:S(2)}) copy-start(s32[128]{0:T(128)} %param.8) | copy-start | bytes 1540
Sparse Core Ops, SparseCore 0:
  17.6 40.5 all-gather.1
  318.4 67.9 reduce-scatter.1
where the time goes:
time: 396 us; the launch traced here: 395 us
  waiting for transfers between devices  304 us (77%)
  matrix products  24.7 us (6%)
  local copies, waits for them, and re-layouts  15.9 us (4%)
  starting transfers between devices  14.4 us (4%)
  other arithmetic  13.8 us (3%)
  between operations  13.6 us (3%)
  blocking collectives  8.4 us (2%)
    all_to_all x1, waiting for transfers between devices, body(): lax.all_to_all(sent_terms, 'tile', split_axis=1, concat_axis=1, tiled=True)  135 us
    all_to_all x1, waiting for transfers between devices, body(): lax.all_to_all(reply_rows, 'tile', split_axis=1, concat_axis=1, tiled=True)  70.8 us
    reduce_scatter x1, waiting for transfers between devices, body(): lax.psum_scatter(jnp.einsum('ct,mtk->cmk', picked, backward_terms, precis...  68.2 us
    all_gather x1, waiting for transfers between devices, body(): gathered = lax.all_gather(member_deviations, 'tile', axis=1, tiled=True)  30 us
    psum x1, blocking collectives, body(): ensemble_sum = lax.psum(local_sum, 'mem')  8.4 us
    dot_general x1, matrix products, body(): jnp.einsum('ds,msk->mdk', row_match, got_terms, precision=lax.Precision.H...  8.12 us
  transfers between devices with their start and end apart: 5, of which 4 were waited for; matrix products, arithmetic and copies ran while one was open for 7% of the time, Pallas kernels for 0%

commit v1 on v0

--- a/solution.py
+++ b/solution.py
@@ -61,7 +61,12 @@
     obs_weight = (precision_weight.astype(jnp.float32) / 8.0).reshape(SOUND_DEV, tile_size)
     weighted = (obs_weight[None, :, :] * (modelled - targets)).astype(jnp.bfloat16)
     reply_rows = jnp.take(weighted, jnp.minimum(got_rows, SOUND_DEV - 1), axis=1)
-    returned = lax.all_to_all(reply_rows, "tile", split_axis=1, concat_axis=1, tiled=True)
+    returned = jnp.concatenate(
+        lax.all_to_all(
+            jnp.stack(jnp.split(reply_rows, lax.axis_size("tile"), axis=1)), "tile", 0, 0
+        ),
+        axis=1,
+    )
     residual_tiles = jnp.take(returned, row_slot, axis=1)
     backward_terms = jnp.einsum(
         "mtr,trk->mtk", residual_tiles, footprints, preferred_element_type=jnp.float32

time: 396 us -> 401 us (1.013)
  local copies, waits for them, and re-layouts: 15.9 us -> 22.2 us
    unnamed x8 -> x15, local copies, waits for them, and re-layouts: 1.81 us -> 7.25 us
where the time goes in v1:
time: 401 us; the launch traced here: 400 us
  waiting for transfers between devices  304 us (76%)
  matrix products  24.7 us (6%)
  local copies, waits for them, and re-layouts  22.2 us (6%)
  starting transfers between devices  14.8 us (4%)
  between operations  13.6 us (3%)
  other arithmetic  12.5 us (3%)
  blocking collectives  8.4 us (2%)
    all_to_all x1, waiting for transfers between devices, body(): lax.all_to_all(sent_terms, 'tile', split_axis=1, concat_axis=1, tiled=True)  135 us
    all_to_all x1, waiting for transfers between devices, body(): lax.all_to_all(jnp.stack(jnp.split(reply_rows, lax.axis_size('tile'), axi...  70.6 us
    reduce_scatter x1, waiting for transfers between devices, body(): lax.psum_scatter(jnp.einsum('ct,mtk->cmk', picked, backward_terms, precis...  68.3 us
    all_gather x1, waiting for transfers between devices, body(): gathered = lax.all_gather(member_deviations, 'tile', axis=1, tiled=True)  30 us
    psum x1, blocking collectives, body(): ensemble_sum = lax.psum(local_sum, 'mem')  8.4 us
    dot_general x1, matrix products, body(): jnp.einsum('ds,msk->mdk', row_match, got_terms, precision=lax.Precision.H...  8.12 us
  transfers between devices with their start and end apart: 5, of which 4 were waited for; matrix products, arithmetic and copies ran while one was open for 7% of the time, Pallas kernels for 0%

profile of v1, /device:TPU:0, one launch (start us, length us, event | category | flops | bytes accessed | tf_op | source)
XLA Modules:
  0.0 400.1 jit_solution(11962337496920211988)
XLA Ops:
  6.5 0.9 convert_reduce_fusion
  7.5 8.4 %psum.7 = f32[1024]{0:T(1024)S(1)} all-reduce(f32[1024]{0:T(1024)S(1)} %convert_reduce_fusion), channel_id=1, replica_groups=mesh['tile'=8,'mem'=4] {'mem'}, use_global_device_ids=true, to_apply=%region_4.5 | all-reduce | flops 1024 | bytes 8192 | tf_op jit(solution)/shard_map/psum | solution.py:37
  15.9 1.6 fusion.32
  18.6 1.6 gather_fusion
  21.0 5.8 %all-to-all-start = ((s32[1,8,24]{2,0,1:T(1,128)}), s32[1,8,24]{2,0,1:T(1,128)S(1)}, u32[]{:S(2)}, u32[]{:S(2)}) async-start(s32[1,8,24]{2,0,1:T(1,128)} %bitcast.3), calls=%async_computation | async-start | bytes 8192 | tf_op jit(solution)/shard_map/all_to_all | solution.py:55
  28.2 30.0 %all-gather.2.cloned.1.call-done = bf16[64,8192]{1,0:T(8,128)(2,1)} async-done(((bf16[64,1024]{1,0:T(8,128)(2,1)}), bf16[64,8192]{1,0:T(8,128)(2,1)}) %all-gather.2.cloned.1.call-update) | async-done | bytes 1048592 | tf_op jit(solution)/shard_map/all_gather | solution.py:46
  58.2 1.5 copy_bitcast_fusion
  59.7 1.0 gather_fusion.1
  60.7 7.0 %convolution_bitcast_fusion.1 = f32[64,128,128]{2,0,1:T(8,128)} fusion(bf16[128,128,128]{2,1,0:T(8,128)(2,1)} %param.6, bf16[128,64,128]{2,1,0:T(8,128)(2,1)S(1)} %gather_fusion.1, pred[128]{0:T(512)(128)(4,1)S(1)} %compare_and_fusion), kind=kOutput, calls=%fused_computation.12 | convolution fusion | flops 269484032 | bytes 10485888 | tf_op jit(solution)/shard_map/mtk,trk->mtr/dot_general | solution.py:48
  67.7 5.8 %gather_fusion.2 = f32[192,64,128]{2,1,0:T(8,128)} fusion(f32[64,128,128]{2,0,1:T(8,128)} %convolution_bitcast_fusion.1, s32[1024]{0:T(1024)S(1)} %pad_clamp_fusion.3), kind=kCustom, calls=%fused_computation.2 | custom fusion | bytes 12583680 | tf_op jit(solution)/shard_map/jit(_take)/gather | solution.py:25
  73.5 5.4 %select_bitcast_fusion = f32[64,192,128]{2,0,1:T(8,128)} fusion(f32[192,64,128]{2,1,0:T(8,128)} %gather_fusion.2, pred[192]{0:T(512)(128)(4,1)S(1)} %fusion.33, pred[192]{0:T(512)(128)(4,1)S(1)} %compare_and_fusion.1), kind=kLoop, calls=%fused_computation.7 | loop fusion | flops 3145728 | bytes 12583296 | tf_op jit(solution)/shard_map/jit(_where)/select_n | solution.py:26
  79.0 5.1 %all-to-all-start.1 = ((f32[64,192,128]{2,0,1:T(8,128)}), f32[64,192,128]{2,0,1:T(8,128)}, u32[]{:S(2)}, u32[]{:S(2)}) async-start(f32[64,192,128]{2,0,1:T(8,128)} %select_bitcast_fusion), calls=%async_computation.1 | async-start | bytes 12582912 | tf_op jit(solution)/shard_map/all_to_all | solution.py:54
  85.6 135.0 %all-to-all-done.1 = f32[64,192,128]{2,0,1:T(8,128)} async-done(((f32[64,192,128]{2,0,1:T(8,128)}), f32[64,192,128]{2,0,1:T(8,128)}, u32[]{:S(2)}, u32[]{:S(2)}) %all-to-all-start.1) | async-done | bytes 6291488 | tf_op jit(solution)/shard_map/all_to_all | solution.py:54
  220.6 8.1 %fusion.19 = bf16[64,16,128]{2,1,0:T(8,128)(2,1)S(1)} fusion(f32[64,16,128]{2,1,0:T(8,128)S(1)} %bitcast.85, f32[64,192,128]{2,0,1:T(8,128)} %all-to-all-done.1, f32[16,128]{1,0:T(8,128)S(1)} %multiply_bitcast_fusion, s32[192]{0:T(256)S(1)} %squeeze.3), kind=kOutput, calls=%fused_computation.22 | convolution fusion | flops 302386176 | bytes 7086848 | tf_op jit(solution)/shard_map/ds,msk->mdk/dot_general | solution.py:59
  228.7 1.2 gather_fusion.3
  233.0 0.8 fusion.28
  234.6 0.8 fusion.26
  236.9 3.6 all-to-all-start.2
  240.9 70.6 %all-to-all-done.2 = bf16[8,64,24,128]{3,1,2,0:T(8,128)(2,1)S(1)} async-done(((bf16[8,64,24,128]{3,1,2,0:T(8,128)(2,1)}), bf16[8,64,24,128]{3,1,2,0:T(8,128)(2,1)S(1)}, u32[]{:S(2)}, u32[]{:S(2)}) %all-to-all-start.2) | async-done | bytes 3145760 | tf_op jit(solution)/shard_map/all_to_all | solution.py:65
  311.5 2.2 gather_fusion.4
  313.6 4.1 %convolution_bitcast_fusion = f32[64,128,128]{2,0,1:T(8,128)S(1)} fusion(bf16[128,128,128]{2,1,0:T(8,128)(2,1)} %param.6, bf16[128,64,128]{2,1,0:T(8,128)(2,1)} %gather_fusion.4, pred[128]{0:T(512)(128)(4,1)S(1)} %get-tuple-element.7), kind=kOutput, calls=%fused_computation.11 | convolution fusion | flops 269484032 | bytes 10485888 | tf_op jit(solution)/shard_map/mtr,trk->mtk/dot_general | solution.py:71
  317.7 5.5 %fusion.2 = f32[64,64,128]{2,0,1:T(8,128)} fusion(f32[64,128,128]{2,0,1:T(8,128)S(1)} %convolution_bitcast_fusion, s32[128]{0:T(128)S(1)} %copy-done.2), kind=kOutput, calls=%fused_computation.8 | convolution fusion | flops 805314560 | bytes 6291968 | tf_op jit(solution)/shard_map/ct,mtk->cmk/dot_general | solution.py:78
  323.2 68.3 %reduce-scatter.2.cloned.1.call-done = f32[8,64,128]{2,0,1:T(8,128)} async-done(((f32[64,64,128]{2,0,1:T(8,128)}), f32[8,64,128]{2,0,1:T(8,128)}) %reduce-scatter.2.cloned.1.call-update) | async-done | bytes 262160 | tf_op jit(solution)/shard_map/reduce_scatter | solution.py:77
  391.6 1.7 copy.55
  (46 shorter events, 10.6 us)
Async XLA Ops:
  6.5 51.7 %all-gather.2.cloned.1.call-start = ((), (), s32[]{:S(2)}) async-start(), calls=%async_computation.4 | async-start | bytes 1179648 | tf_op jit(solution)/shard_map/all_gather | solution.py:46
  21.0 57.9 %all-to-all-start = ((s32[1,8,24]{2,0,1:T(1,128)}), s32[1,8,24]{2,0,1:T(1,128)S(1)}, u32[]{:S(2)}, u32[]{:S(2)}) async-start(s32[1,8,24]{2,0,1:T(1,128)} %bitcast.3), calls=%async_computation | async-start | bytes 8192 | tf_op jit(solution)/shard_map/all_to_all | solution.py:55
  79.0 5.1 %copy-start = (f32[64,2048]{1,0:T(8,128)S(1)}, f32[64,2048]{1,0:T(8,128)}, u32[]{:S(2)}) copy-start(f32[64,2048]{1,0:T(8,128)} %param.10) | copy-start | bytes 1572868
  79.0 5.2 %copy-start.1 = (s32[2048]{0:T(1024)S(1)}, s32[2048]{0:T(1024)}, u32[]{:S(2)}) copy-start(s32[2048]{0:T(1024)} %param.11) | copy-start | bytes 24580
  79.0 141.6 %all-to-all-start.1 = ((f32[64,192,128]{2,0,1:T(8,128)}), f32[64,192,128]{2,0,1:T(8,128)}, u32[]{:S(2)}, u32[]{:S(2)}) async-start(f32[64,192,128]{2,0,1:T(8,128)} %select_bitcast_fusion), calls=%async_computation.1 | async-start | bytes 12582912 | tf_op jit(solution)/shard_map/all_to_all | solution.py:54
  236.9 74.5 %all-to-all-start.2 = ((bf16[8,64,24,128]{3,1,2,0:T(8,128)(2,1)}), bf16[8,64,24,128]{3,1,2,0:T(8,128)(2,1)S(1)}, u32[]{:S(2)}, u32[]{:S(2)}) async-start(bf16[8,64,24,128]{3,1,2,0:T(8,128)(2,1)} %fusion.24), calls=%async_computation.2 | async-start | bytes 6291456 | tf_op jit(solution)/shard_map/all_to_all | solution.py:65
  240.6 151.0 %reduce-scatter.2.cloned.1.call-start = ((), (), s32[]{:S(2)}) async-start(), calls=%async_computation.5 | async-start | bytes 2359296 | tf_op jit(solution)/shard_map/reduce_scatter | solution.py:77
  313.6 4.1 %copy-start.2 = (s32[128]{0:T(128)S(1)}, s32[128]{0:T(128)}, u32[]{:S(2)}) copy-start(s32[128]{0:T(128)} %param.8) | copy-start | bytes 1540
Sparse Core Ops, SparseCore 0:
  17.6 40.5 all-gather.1
  323.3 68.1 reduce-scatter.1
